TPU v7x, 32 devices: a whole 2x2x4 slice. The times are simulated.
32 devices in a mesh: rep: 1, fsdp: 32 (over z, y, x, core).
Axes of the slice: x: 2, y: 2, z: 4, core: 2. Of those that a mesh axis runs over, the one named last changes fastest.
Arguments:
- grads: bfloat16 [1, 24, 1280, 1280], P('rep', None, 'fsdp'), as said below
- group_counts: int32 [2], replicated, may hold values from 1 to 18, 24 in all
- owners: int32 [24], replicated, may hold values from 0 to 31, as said below
- left_stat: float32 [32, 1280, 1280], P('fsdp', 'rep'), may hold values from -4 to 4
- right_stat: float32 [32, 1280, 1280], P('fsdp', 'rep'), may hold values from -4 to 4
- left_root: bfloat16 [32, 1280, 1280], P('fsdp', 'rep'), as said below
- right_root: bfloat16 [32, 1280, 1280], P('fsdp', 'rep'), as said below
Outputs:
- left_new: float32 [32, 1280, 1280], P('fsdp', 'rep')
- right_new: float32 [32, 1280, 1280], P('fsdp', 'rep')
- update: bfloat16 [24, 1280, 1280], P(None, ('rep', 'fsdp'))
Inputs may be any that keep to these rules, and one draw needn't show every extreme that they name: `grads`: block gradients of every replica group, real-valued. `owners`: no slot is named by two blocks. `group_counts`: the counts add up to 24. `left_root`: Symmetric, with a positive diagonal of about 0.5 to 2, each entry within a small symmetric perturbation of that range, and off-diagonal entries much smaller than the diagonal. `right_root`: Symmetric, with a positive diagonal of about 0.5 to 2, each entry within a small symmetric perturbation of that range, and off-diagonal entries much smaller than the diagonal.
All inputs are finite; a program needn't handle non-finite values.
Results may differ from a plain program's by a relative error of at most 0.00065.
The roundings to bfloat16 on the way count: a program that leaves them out, or rounds other values in their place, can miss the bound.
Values may be sent and summed in bfloat16 or wider, within the bound.
A program may use at most 128 MiB of HBM per device.

v0:
```python
import jax
import jax.numpy as jnp
from jax import lax
from jax.sharding import PartitionSpec as P

BETA = 0.95
EPSILON = 1e-06


def on_device(grads, group_counts, owners, left_stat, right_stat, left_root, right_root):
    slots = lax.axis_size("fsdp")
    width = left_stat.shape[2]
    half_rows = left_stat.shape[1]
    slot_ids = jnp.arange(slots, dtype=jnp.int32)
    placing = (owners[:, None] == slot_ids[None, :]).astype(jnp.bfloat16)
    local = grads[0]
    summed = lax.psum(local, "rep").astype(jnp.float32).astype(jnp.bfloat16)
    slotted = jnp.einsum("bs,brc->src", placing, summed, preferred_element_type=jnp.float32).astype(
        jnp.bfloat16
    )
    block = lax.all_to_all(slotted, "fsdp", split_axis=0, concat_axis=1, tiled=True)[0]
    first = lax.axis_index("rep") * half_rows
    mine = lax.dynamic_slice_in_dim(block, first, half_rows, 0)
    columns = lax.dynamic_slice_in_dim(block, first, half_rows, 1)
    coef = (1.0 - BETA) / width
    left_gram = jnp.dot(mine, block.T, preferred_element_type=jnp.float32)
    right_gram = lax.dot_general(
        columns, block, (((0,), (0,)), ((), ())), preferred_element_type=jnp.float32
    )
    left_new = BETA * left_stat[0] + coef * left_gram
    right_new = BETA * right_stat[0] + coef * right_gram
    whole_root = lax.all_gather(right_root, "rep", axis=1, tiled=True)[0]
    halfway = jnp.dot(left_root[0], block, preferred_element_type=jnp.float32).astype(jnp.bfloat16)
    precond = jnp.dot(halfway, whole_root, preferred_element_type=jnp.float32)
    ends = jnp.cumsum(group_counts)
    starts = ends - group_counts
    block_ids = jnp.arange(owners.shape[0], dtype=jnp.int32)
    member = (
        (block_ids[:, None] >= starts[None, :]) & (block_ids[:, None] < ends[None, :])
    ).astype(jnp.float32)
    owned_here = (owners == lax.axis_index("fsdp")).astype(jnp.float32)
    my_groups = jnp.sum(owned_here[:, None] * member, axis=0)
    mine_float = mine.astype(jnp.float32)
    grad_part = my_groups * jnp.sum(mine_float * mine_float)
    prec_part = my_groups * jnp.sum(precond * precond)
    grad_sq, prec_sq = lax.psum((grad_part, prec_part), ("rep", "fsdp"))
    ratio = jnp.sum(my_groups * jnp.sqrt((grad_sq + EPSILON) / (prec_sq + EPSILON)))
    scaled = (precond * ratio).astype(jnp.bfloat16)
    returned = lax.all_to_all(scaled[None], "fsdp", split_axis=1, concat_axis=0, tiled=True)
    update = jnp.einsum(
        "bs,srw->brw", placing, returned, preferred_element_type=jnp.float32
    ).astype(jnp.bfloat16)
    return (left_new[None], right_new[None], update)


def solution(mesh):
    in_specs = (
        P("rep", None, "fsdp", None),
        P(),
        P(),
        P("fsdp", "rep", None),
        P("fsdp", "rep", None),
        P("fsdp", "rep", None),
        P("fsdp", "rep", None),
    )
    out_specs = (P("fsdp", "rep", None), P("fsdp", "rep", None), P(None, ("rep", "fsdp"), None))
    return jax.shard_map(
        on_device, mesh=mesh, in_specs=in_specs, out_specs=out_specs, check_vma=False
    )
```

profile of v0, /device:TPU:0, one launch (start us, length us, event | category | flops | bytes accessed | tf_op | source)
XLA Modules:
  0.0 352.4 jit_solution(14322082575381790667)
XLA Ops:
  0.6 0.0 copy-start
  0.6 3.0 convolution_convert_fusion.1
  3.6 3.5 copy.33
  7.1 0.0 copy-start.3
  7.1 0.0 copy-start.2
  7.1 7.9 %all-to-all-start = ((bf16[32,40,1280]{2,1,0:T(8,128)(2,1)}), bf16[32,40,1280]{2,1,0:T(8,128)(2,1)}, u32[]{:S(2)}, u32[]{:S(2)}) async-start(bf16[32,40,1280]{2,1,0:T(8,128)(2,1)} %copy.33), calls=%async_computation | async-start | bytes 6553600 | tf_op jit(solution)/shard_map/all_to_all | solution.py:21
  15.1 0.0 copy-done.3
  15.1 0.2 reduce-window.8
  15.2 0.0 copy-done.2
  15.3 0.2 fusion.18
  15.4 73.3 %all-to-all-done = bf16[32,40,1280]{2,1,0:T(8,128)(2,1)} async-done(((bf16[32,40,1280]{2,1,0:T(8,128)(2,1)}), bf16[32,40,1280]{2,1,0:T(8,128)(2,1)}, u32[]{:S(2)}, u32[]{:S(2)}) %all-to-all-start) | async-done | bytes 3276832 | tf_op jit(solution)/shard_map/all_to_all | solution.py:21
  88.7 0.0 copy-done
  88.7 23.3 %multiply_reduce_fusion = (f32[]{:T(128)}, f32[1280,1280]{1,0:T(8,128)}) fusion(bf16[1,1280,1280]{2,1,0:T(8,128)(2,1)S(1)} %copy-done, bf16[1280,1280]{1,0:T(8,128)(2,1)} %bitcast.3, bf16[1,1280,1280]{2,1,0:T(8,128)(2,1)} %param.12), kind=kOutput, calls=%fused_computation.9 | convolution fusion | flops 8393523200 | bytes 16384004 | tf_op jit(solution)/shard_map/dot_general | solution.py:34
  112.0 4.2 %multiply_reduce_fusion.1 = f32[]{:T(128)} fusion(bf16[32,40,1280]{2,1,0:T(8,128)(2,1)} %all-to-all-done), kind=kLoop, calls=%fused_computation.10 | loop fusion | flops 4915199 | bytes 3276804 | tf_op jit(solution)/shard_map/reduce_sum | solution.py:44
  116.2 1.3 broadcast_multiply_fusion.1
  117.5 38.1 %all-reduce = (f32[2]{0:T(128)S(1)}, f32[2]{0:T(128)S(1)}) all-reduce(f32[2]{0:T(128)S(1)} %get-tuple-element.21, f32[2]{0:T(128)S(1)} %get-tuple-element.20), channel_id=1, replica_groups=mesh['rep'=1,'fsdp'=32] {'rep','fsdp'}, use_global_device_ids=true, to_apply=%region_5.6 | all-reduce | flops 4 | bytes 32 | tf_op jit(solution)/shard_map/psum | solution.py:46
  155.6 0.6 multiply_reduce_fusion.2
  156.3 4.0 %fusion.5 = bf16[1,1280,1280]{2,1,0:T(8,128)(2,1)S(1)} fusion(f32[1280,1280]{1,0:T(8,128)} %get-tuple-element.23, f32[]{:T(128)} %multiply_reduce_fusion.2), kind=kLoop, calls=%fused_computation.13 | loop fusion | flops 3276800 | bytes 9830404 | tf_op jit(solution)/shard_map/broadcast_in_dim | solution.py:49
  160.3 21.5 %copy.43 = bf16[1,1280,1280]{2,0,1:T(2,128)(2,1)} copy(bf16[1,1280,1280]{2,1,0:T(8,128)(2,1)S(1)} %fusion.5) | data formatting | bytes 6553600 | tf_op jit(solution)/shard_map/broadcast_in_dim | solution.py:49
  181.7 0.5 broadcast.28
  182.2 69.6 %reduce.1 = bf16[1280,1280]{1,0:T(8,128)(2,1)S(1)} reduce(bf16[1280,1,1280]{2,1,0:T(2,128)(2,1)} %bitcast.49, bf16[]{:T(256)} %broadcast.28), dimensions={1}, to_apply=%bitcast.48.reduce_sub_computation | reduce | bytes 6553602
  251.8 2.5 reshape.47
  254.3 5.2 %all-to-all-start.1 = ((bf16[32,2,25600]{2,1,0:T(2,128)(2,1)}), bf16[32,2,25600]{2,1,0:T(2,128)(2,1)S(1)}, u32[]{:S(2)}, u32[]{:S(2)}) async-start(bf16[32,2,25600]{2,1,0:T(2,128)(2,1)} %reshape.47), calls=%async_computation.1 | async-start | bytes 6553600 | tf_op jit(solution)/shard_map/all_to_all | solution.py:49
  259.6 12.2 %fusion.1 = f32[1,1280,1280]{2,1,0:T(8,128)} fusion(bf16[1280,1280]{1,0:T(8,128)(2,1)} %bitcast.3, f32[1,1280,1280]{2,1,0:T(8,128)} %param.10), kind=kOutput, calls=%fused_computation.2 | convolution fusion | flops 4199219200 | bytes 16384000 | tf_op jit(solution)/shard_map/dot_general | solution.py:26
  271.8 12.3 %fusion.4 = f32[1,1280,1280]{2,1,0:T(8,128)} fusion(bf16[32,40,1280]{2,1,0:T(8,128)(2,1)} %all-to-all-done, f32[1,1280,1280]{2,1,0:T(8,128)} %param.11), kind=kOutput, calls=%fused_computation.6 | convolution fusion | flops 4199219200 | bytes 16384000 | tf_op jit(solution)/shard_map/dot_general | solution.py:27
  284.1 49.6 %all-to-all-done.1 = bf16[32,2,25600]{2,1,0:T(2,128)(2,1)S(1)} async-done(((bf16[32,2,25600]{2,1,0:T(2,128)(2,1)}), bf16[32,2,25600]{2,1,0:T(2,128)(2,1)S(1)}, u32[]{:S(2)}, u32[]{:S(2)}) %all-to-all-start.1) | async-done | bytes 3276832 | tf_op jit(solution)/shard_map/all_to_all | solution.py:49
  333.7 12.3 %reshape.48 = bf16[1280,1,1280]{2,1,0:T(2,128)(2,1)} reshape(bf16[32,2,25600]{2,1,0:T(2,128)(2,1)S(1)} %all-to-all-done.1) | data formatting | bytes 6553600
  346.0 3.4 copy.37
  349.4 0.0 copy-start.1
  349.4 0.9 convolution_convert_fusion.2
  350.2 1.9 copy.36
  352.1 0.0 copy-done.1
  (2 shorter events, 0.0 us)
Async XLA Ops:
  0.6 88.1 %copy-start = (bf16[1,1280,1280]{2,1,0:T(8,128)(2,1)S(1)}, bf16[1,1280,1280]{2,1,0:T(8,128)(2,1)}, u32[]{:S(2)}) copy-start(bf16[1,1280,1280]{2,1,0:T(8,128)(2,1)} %param.13) | copy-start | bytes 9830404
  7.1 7.9 %copy-start.3 = (s32[2]{0:T(128)S(1)}, s32[2]{0:T(128)}, u32[]{:S(2)}) copy-start(s32[2]{0:T(128)} %param.8) | copy-start | bytes 28
  7.1 8.1 %copy-start.2 = (s32[24]{0:T(128)S(1)}, s32[24]{0:T(128)}, u32[]{:S(2)}) copy-start(s32[24]{0:T(128)} %param.9) | copy-start | bytes 292
  7.1 81.6 %all-to-all-start = ((bf16[32,40,1280]{2,1,0:T(8,128)(2,1)}), bf16[32,40,1280]{2,1,0:T(8,128)(2,1)}, u32[]{:S(2)}, u32[]{:S(2)}) async-start(bf16[32,40,1280]{2,1,0:T(8,128)(2,1)} %copy.33), calls=%async_computation | async-start | bytes 6553600 | tf_op jit(solution)/shard_map/all_to_all | solution.py:21
  254.3 79.4 %all-to-all-start.1 = ((bf16[32,2,25600]{2,1,0:T(2,128)(2,1)}), bf16[32,2,25600]{2,1,0:T(2,128)(2,1)S(1)}, u32[]{:S(2)}, u32[]{:S(2)}) async-start(bf16[32,2,25600]{2,1,0:T(2,128)(2,1)} %reshape.47), calls=%async_computation.1 | async-start | bytes 6553600 | tf_op jit(solution)/shard_map/all_to_all | solution.py:49
  349.4 2.8 copy-start.1
where the time goes:
time: 356 us; the launch traced here: 352 us
  waiting for transfers between devices  123 us (35%)
  other arithmetic  80 us (22%)
  matrix products  51.7 us (15%)
  local copies, waits for them, and re-layouts  45.6 us (13%)
  blocking collectives  38.1 us (11%)
  starting transfers between devices  13.1 us (4%)
    all_to_all x1, waiting for transfers between devices, on_device(): lax.all_to_all(slotted, 'fsdp', split_axis=0, concat_axis=1, tiled=True)[0]  73.3 us
    unnamed x1, other arithmetic  69.6 us
    all_to_all x1, waiting for transfers between devices, on_device(): lax.all_to_all(scaled[None], 'fsdp', split_axis=1, concat_axis=0, tiled=T...  49.6 us
    psum x1, blocking collectives, on_device(): grad_sq, prec_sq = lax.psum((grad_part, prec_part), ('rep', 'fsdp'))  38.1 us
    dot_general x1, matrix products, on_device(): precond = jnp.dot(halfway, whole_root, preferred_element_type=jnp.float32)  23.3 us
    broadcast_in_dim x1, local copies, waits for them, and re-layouts, on_device(): scaled[None]  21.5 us
    unnamed x13, local copies, waits for them, and re-layouts  20.6 us
    dot_general x1, matrix products, on_device(): lax.dot_general(columns, block, (((0,), (0,)), ((), ())), preferred_eleme...  12.3 us
  transfers between devices with their start and end apart: 2, of which 2 were waited for; matrix products, arithmetic and copies ran while one was open for 7% of the time, Pallas kernels for 0%

commit v1 on v0

--- a/solution.py
+++ b/solution.py
@@ -46,7 +46,10 @@
     grad_sq, prec_sq = lax.psum((grad_part, prec_part), ("rep", "fsdp"))
     ratio = jnp.sum(my_groups * jnp.sqrt((grad_sq + EPSILON) / (prec_sq + EPSILON)))
     scaled = (precond * ratio).astype(jnp.bfloat16)
-    returned = lax.all_to_all(scaled[None], "fsdp", split_axis=1, concat_axis=0, tiled=True)
+    block_2 = scaled[None]
+    cells = jnp.split(block_2, lax.axis_size("fsdp"), axis=1)
+    received = lax.all_to_all(jnp.stack(cells), "fsdp", 0, 0)
+    returned = jnp.concatenate(received, axis=0)
     update = jnp.einsum(
         "bs,srw->brw", placing, returned, preferred_element_type=jnp.float32
     ).astype(jnp.bfloat16)

time: 356 us -> 265 us (0.74); the launches traced: 352 us -> 265 us
  other arithmetic: 80 us -> 10.5 us
  local copies, waits for them, and re-layouts: 45.6 us -> 26.1 us
    unnamed x1 -> x0, other arithmetic: 69.6 us -> none
    broadcast_in_dim x1 -> x0, local copies, waits for them, and re-layouts: 21.5 us -> none  [on_device(): scaled[None]]
    unnamed x13 -> x38, local copies, waits for them, and re-layouts: 20.6 us -> 21.9 us
  transfers between devices with their start and end apart: 2 -> 2, of which waited for: 2 -> 2; matrix products, arithmetic and copies ran while one was open for 7% -> 9% of each run, Pallas kernels for 0% -> 0%
where the time goes in v1:
time: 265 us
  waiting for transfers between devices  123 us (46%)
  matrix products  53.6 us (20%)
  blocking collectives  38.1 us (14%)
  local copies, waits for them, and re-layouts  26.1 us (10%)
  starting transfers between devices  12.7 us (5%)
  other arithmetic  10.5 us (4%)
    all_to_all x1, waiting for transfers between devices, on_device(): lax.all_to_all(slotted, 'fsdp', split_axis=0, concat_axis=1, tiled=True)[0]  73.6 us
    all_to_all x1, waiting for transfers between devices, on_device(): received = lax.all_to_all(jnp.stack(cells), 'fsdp', 0, 0)  49.6 us
    psum x1, blocking collectives, on_device(): grad_sq, prec_sq = lax.psum((grad_part, prec_part), ('rep', 'fsdp'))  38.1 us
    dot_general x1, matrix products, on_device(): precond = jnp.dot(halfway, whole_root, preferred_element_type=jnp.float32)  23.4 us
    unnamed x38, local copies, waits for them, and re-layouts  21.9 us
    dot_general x1, matrix products, on_device(): lax.dot_general(columns, block, (((0,), (0,)), ((), ())), preferred_eleme...  12.3 us
    dot_general x1, matrix products, on_device(): left_gram = jnp.dot(mine, block.T, preferred_element_type=jnp.float32)  12.2 us
    all_to_all x1, starting transfers between devices, on_device(): lax.all_to_all(slotted, 'fsdp', split_axis=0, concat_axis=1, tiled=True)[0]  7.62 us
  transfers between devices with their start and end apart: 2, of which 2 were waited for; matrix products, arithmetic and copies ran while one was open for 9% of the time, Pallas kernels for 0%

profile of v1, /device:TPU:0, one launch (start us, length us, event | category | flops | bytes accessed | tf_op | source)
XLA Modules:
  0.0 264.9 jit_solution(521083990299174122)
XLA Ops:
  0.6 0.0 copy-start
  0.6 3.0 %convolution_convert_fusion.1 = bf16[32,40,1280]{2,0,1:T(8,128)(2,1)S(1)} fusion(bf16[24,40,1280]{2,1,0:T(8,128)(2,1)} %bitcast.173, s32[24]{0:T(128)} %param.9), kind=kOutput, calls=%fused_computation.11 | convolution fusion | flops 80282368 | bytes 5734496 | tf_op jit(solution)/shard_map/bs,brc->src/dot_general | solution.py:18
  3.6 3.5 %copy.28 = bf16[32,40,1280]{2,1,0:T(8,128)(2,1)} copy(bf16[32,40,1280]{2,0,1:T(8,128)(2,1)S(1)} %convolution_convert_fusion.1) | data formatting | bytes 6553600 | tf_op jit(solution)/shard_map/convert_element_type | solution.py:18
  7.1 0.0 copy-start.2
  7.1 0.0 copy-start.1
  7.1 7.6 %all-to-all-start = ((bf16[32,40,1280]{2,1,0:T(8,128)(2,1)}), bf16[32,40,1280]{2,1,0:T(8,128)(2,1)}, u32[]{:S(2)}, u32[]{:S(2)}) async-start(bf16[32,40,1280]{2,1,0:T(8,128)(2,1)} %copy.28), calls=%async_computation | async-start | bytes 6553600 | tf_op jit(solution)/shard_map/all_to_all | solution.py:21
  14.8 0.0 copy-done.2
  14.8 0.2 reduce-window.8
  15.0 0.0 copy-done.1
  15.0 0.2 fusion.50
  15.2 73.6 %all-to-all-done = bf16[32,40,1280]{2,1,0:T(8,128)(2,1)} async-done(((bf16[32,40,1280]{2,1,0:T(8,128)(2,1)}), bf16[32,40,1280]{2,1,0:T(8,128)(2,1)}, u32[]{:S(2)}, u32[]{:S(2)}) %all-to-all-start) | async-done | bytes 3276832 | tf_op jit(solution)/shard_map/all_to_all | solution.py:21
  88.7 0.0 copy-done
  88.7 23.4 %multiply_reduce_fusion = (f32[]{:T(128)}, f32[1280,1280]{1,0:T(8,128)}) fusion(bf16[1,1280,1280]{2,1,0:T(8,128)(2,1)S(1)} %copy-done, bf16[1280,1280]{1,0:T(8,128)(2,1)} %bitcast.3, bf16[1,1280,1280]{2,1,0:T(8,128)(2,1)} %param.12), kind=kOutput, calls=%fused_computation.9 | convolution fusion | flops 8393523200 | bytes 16384004 | tf_op jit(solution)/shard_map/dot_general | solution.py:34
  112.1 4.2 %multiply_reduce_fusion.1 = f32[]{:T(128)} fusion(bf16[32,40,1280]{2,1,0:T(8,128)(2,1)} %all-to-all-done), kind=kLoop, calls=%fused_computation.10 | loop fusion | flops 4915199 | bytes 3276804 | tf_op jit(solution)/shard_map/reduce_sum | solution.py:44
  116.3 1.3 broadcast_multiply_fusion.1
  117.6 38.1 %all-reduce = (f32[2]{0:T(128)S(1)}, f32[2]{0:T(128)S(1)}) all-reduce(f32[2]{0:T(128)S(1)} %get-tuple-element.18, f32[2]{0:T(128)S(1)} %get-tuple-element.17), channel_id=1, replica_groups=mesh['rep'=1,'fsdp'=32] {'rep','fsdp'}, use_global_device_ids=true, to_apply=%region_5.6 | all-reduce | flops 4 | bytes 32 | tf_op jit(solution)/shard_map/psum | solution.py:46
  155.7 0.6 multiply_reduce_fusion.2
  156.3 4.0 %fusion.5 = bf16[1,1280,1280]{2,1,0:T(8,128)(2,1)S(1)} fusion(f32[1280,1280]{1,0:T(8,128)} %get-tuple-element.20, f32[]{:T(128)} %multiply_reduce_fusion.2), kind=kLoop, calls=%fused_computation.13 | loop fusion | flops 3276800 | bytes 9830404 | tf_op jit(solution)/shard_map/broadcast_in_dim | solution.py:49
  160.3 0.6 fusion.44
  160.9 0.7 fusion.43
  161.6 0.6 fusion.42
  162.2 0.7 fusion.41
  162.9 0.6 fusion.40
  163.5 0.6 fusion.39
  164.2 0.6 fusion.38
  164.8 0.6 fusion.37
  165.5 0.6 fusion.36
  166.1 0.6 fusion.35
  166.8 0.7 fusion.34
  167.4 0.6 fusion.33
  168.1 0.6 fusion.32
  168.7 0.6 fusion.31
  169.3 0.7 fusion.30
  170.0 0.6 fusion.29
  170.6 0.6 fusion.28
  171.3 0.7 fusion.27
  171.9 0.7 fusion.26
  172.6 0.6 fusion.25
  173.2 0.6 fusion.24
  173.9 0.6 fusion.23
  174.5 0.6 fusion.22
  175.1 0.6 fusion.21
  175.8 0.6 fusion.20
  176.4 0.7 fusion.19
  177.1 0.7 fusion.18
  177.7 0.7 fusion.17
  178.4 0.6 fusion.16
  179.0 0.6 fusion.15
  179.7 0.7 fusion.14
  180.3 0.6 fusion.13
  181.0 5.1 %all-to-all-start.1 = ((bf16[32,1,40,1280]{3,2,1,0:T(8,128)(2,1)}), bf16[32,1,40,1280]{3,2,1,0:T(8,128)(2,1)}, u32[]{:S(2)}, u32[]{:S(2)}) async-start(bf16[32,1,40,1280]{3,2,1,0:T(8,128)(2,1)} %fusion.13), calls=%async_computation.1 | async-start | bytes 6553600 | tf_op jit(solution)/shard_map/all_to_all | solution.py:51
  186.1 12.2 %fusion.1 = f32[1,1280,1280]{2,1,0:T(8,128)} fusion(bf16[1280,1280]{1,0:T(8,128)(2,1)} %bitcast.3, f32[1,1280,1280]{2,1,0:T(8,128)} %param.10), kind=kOutput, calls=%fused_computation.2 | convolution fusion | flops 4199219200 | bytes 16384000 | tf_op jit(solution)/shard_map/dot_general | solution.py:26
  198.3 12.3 %fusion.4 = f32[1,1280,1280]{2,1,0:T(8,128)} fusion(bf16[32,40,1280]{2,1,0:T(8,128)(2,1)} %all-to-all-done, f32[1,1280,1280]{2,1,0:T(8,128)} %param.11), kind=kOutput, calls=%fused_computation.6 | convolution fusion | flops 4199219200 | bytes 16384000 | tf_op jit(solution)/shard_map/dot_general | solution.py:27
  210.6 49.6 %all-to-all-done.1 = bf16[32,1,40,1280]{3,2,1,0:T(8,128)(2,1)} async-done(((bf16[32,1,40,1280]{3,2,1,0:T(8,128)(2,1)}), bf16[32,1,40,1280]{3,2,1,0:T(8,128)(2,1)}, u32[]{:S(2)}, u32[]{:S(2)}) %all-to-all-start.1) | async-done | bytes 3276832 | tf_op jit(solution)/shard_map/all_to_all | solution.py:51
  260.2 2.8 %convolution_convert_fusion.2 = bf16[24,40,1280]{2,0,1:T(8,128)(2,1)S(1)} fusion(bf16[32,40,1280]{2,1,0:T(8,128)(2,1)} %bitcast.45, s32[24]{0:T(128)S(1)} %copy-done.1), kind=kOutput, calls=%fused_computation.12 | convolution fusion | flops 79872768 | bytes 5734496 | tf_op jit(solution)/shard_map/bs,srw->brw/dot_general | solution.py:53
  263.0 1.9 copy.30
  (2 shorter events, 0.0 us)
Async XLA Ops:
  0.6 88.1 %copy-start = (bf16[1,1280,1280]{2,1,0:T(8,128)(2,1)S(1)}, bf16[1,1280,1280]{2,1,0:T(8,128)(2,1)}, u32[]{:S(2)}) copy-start(bf16[1,1280,1280]{2,1,0:T(8,128)(2,1)} %param.13) | copy-start | bytes 9830404
  7.1 7.6 %copy-start.2 = (s32[2]{0:T(128)S(1)}, s32[2]{0:T(128)}, u32[]{:S(2)}) copy-start(s32[2]{0:T(128)} %param.8) | copy-start | bytes 28
  7.1 7.8 %copy-start.1 = (s32[24]{0:T(128)S(1)}, s32[24]{0:T(128)}, u32[]{:S(2)}) copy-start(s32[24]{0:T(128)} %param.9) | copy-start | bytes 292
  7.1 81.6 %all-to-all-start = ((bf16[32,40,1280]{2,1,0:T(8,128)(2,1)}), bf16[32,40,1280]{2,1,0:T(8,128)(2,1)}, u32[]{:S(2)}, u32[]{:S(2)}) async-start(bf16[32,40,1280]{2,1,0:T(8,128)(2,1)} %copy.28), calls=%async_computation | async-start | bytes 6553600 | tf_op jit(solution)/shard_map/all_to_all | solution.py:21
  181.0 79.3 %all-to-all-start.1 = ((bf16[32,1,40,1280]{3,2,1,0:T(8,128)(2,1)}), bf16[32,1,40,1280]{3,2,1,0:T(8,128)(2,1)}, u32[]{:S(2)}, u32[]{:S(2)}) async-start(bf16[32,1,40,1280]{3,2,1,0:T(8,128)(2,1)} %fusion.13), calls=%async_computation.1 | async-start | bytes 6553600 | tf_op jit(solution)/shard_map/all_to_all | solution.py:51
